TPU v7x, 256 devices: a whole 4x4x8 slice. The times are simulated.
256 devices in a mesh: blk: 16 (over x_lo, y, core), walk: 16 (over x_hi, z).
Axes of the slice: x: 4 (x_hi: 2, x_lo: 2; x = x_hi * 2 + x_lo), y: 4, z: 8, core: 2. Of those that a mesh axis runs over, the one named last changes fastest.
Arguments:
- walkers: bfloat16 [512, 200, 2048], P(('blk', 'walk')), may hold values from -6 to 6
- inv_intersection: bfloat16 [512, 2, 100, 100], P(('blk', 'walk')), may hold values from -0.625 to 0.625
- rotated_chol: bfloat16 [32, 100, 2048], P('blk'), may hold values from -0.013671875 to 0.013671875
- full_chol: bfloat16 [32, 2048, 2048], P('walk', 'blk'), may hold values from -0.125 to 0.125
- field_noise: float32 [32], replicated, may hold values from -4 to 4
Outputs:
- propagated: bfloat16 [512, 200, 2048], P(('blk', 'walk'))
- force_bias: float32 [512, 32], P(('blk', 'walk'))
- bias_shift: float32 [32], replicated
All inputs are finite; a program needn't handle non-finite values.
Results may differ from a plain program's by a relative error of at most 0.0065.
Values may be sent and summed in bfloat16 or wider, within the bound.
No kernel may reach another device: no remote copies, remote signals or barrier semaphores. Data moves between devices by JAX's collectives and lax.ppermute only.
A program may use at most 128 MiB of HBM per device.

v0:
```python
import functools
import math
import jax
import jax.numpy as jnp
from jax import lax
from jax.sharding import Mesh
from jax.sharding import PartitionSpec as P

BLK = ("blk_0", "blk_1", "blk_2")
WALK = ("walk_0", "walk_1")
BLK_WALK = ("blk_0", "blk_1", "blk_2", "walk_0", "walk_1")
time_root = 0.1


def by_axis(array, axes):
    return functools.reduce(lax.psum, axes, array)


def in_blocks(array, dim, count):
    before, after = (array.shape[:dim], array.shape[dim + 1 :])
    return jnp.moveaxis(array.reshape(*before, count, -1, *after), dim, 0)


def sent_and_summed(array, axis, dim):
    blocks = in_blocks(array, dim, lax.axis_size(axis))
    arrived = lax.all_to_all(blocks, axis, split_axis=0, concat_axis=0, tiled=True)
    return arrived.sum(axis=0)


def sent_to_all(array, axis):
    count = lax.axis_size(axis)
    return lax.all_to_all(
        jnp.broadcast_to(array[None], (count, *array.shape)), axis, 0, 0, tiled=True
    )


def in_order(blocks, dim):
    blocks = jnp.moveaxis(blocks, 0, dim)
    shape = blocks.shape
    return blocks.reshape(*shape[:dim], shape[dim] * shape[dim + 1], *shape[dim + 2 :])


def gather_directly(array, axis, dim):
    blocks = sent_to_all(array, axis)
    return in_order(blocks, dim)


def local(walkers, inv_intersection, rotated_chol, full_chol, field_noise):
    wdev_count, double_rows, orbitals = walkers.shape
    occupied = double_rows // 2
    spins = walkers.reshape(wdev_count, 2, occupied, orbitals)
    theta = jnp.einsum(
        "wsij,wsjp->wip", inv_intersection, spins, preferred_element_type=jnp.float32
    ).astype(jnp.bfloat16)
    flat_theta = theta.reshape(wdev_count, occupied * orbitals)
    piece = lax.all_gather(rotated_chol, BLK, axis=0, tiled=True)
    flat_piece = piece.reshape(piece.shape[0], occupied * orbitals)
    part_bias = lax.dot_general(
        flat_theta, flat_piece, (((1,), (1,)), ((), ())), preferred_element_type=jnp.float32
    )
    total_walkers = wdev_count * lax.axis_size(BLK) * lax.axis_size(WALK)
    bias_shift = by_axis(jnp.sum(part_bias, axis=0), BLK_WALK) / math.sqrt(total_walkers)
    shifted = field_noise - bias_shift
    local_count = full_chol.shape[0]
    local_shift = lax.dynamic_slice_in_dim(shifted, lax.axis_index(WALK) * local_count, local_count)
    partial_value = time_root * jnp.tensordot(
        local_shift, full_chol.astype(jnp.float32), axes=1, precision=lax.Precision.HIGHEST
    )
    narrow = sent_and_summed(partial_value, WALK, 1).astype(jnp.bfloat16)
    row_block = gather_directly(narrow, WALK, 1)
    field = lax.all_gather(row_block, BLK, axis=0, tiled=True)
    current = walkers.reshape(wdev_count * double_rows, orbitals)
    total = current.astype(jnp.float32)
    for order in range(1, 5):
        current = (jnp.dot(current, field, preferred_element_type=jnp.float32) / order).astype(
            jnp.bfloat16
        )
        total = total + current.astype(jnp.float32)
    propagated = total.astype(jnp.bfloat16).reshape(wdev_count, double_rows, orbitals)
    return (propagated, part_bias, bias_shift)


def solution(mesh):
    torus = Mesh(
        mesh.devices.reshape(2, 4, 2, 2, 8), ("blk_0", "blk_1", "blk_2", "walk_0", "walk_1")
    )
    in_specs = (
        P(BLK_WALK, None, None),
        P(BLK_WALK, None, None, None),
        P(BLK, None, None),
        P(WALK, BLK, None),
        P(),
    )
    out_specs = (P(BLK_WALK, None, None), P(BLK_WALK, None), P())
    return jax.shard_map(local, mesh=torus, in_specs=in_specs, out_specs=out_specs, check_vma=False)
```

profile of v0, /device:TPU:1, one launch (start us, length us, event | category | flops | bytes accessed | tf_op | source)
XLA Modules:
  0.0 296.6 jit_solution(11933287155726860161)
XLA Ops:
  7.2 2.4 copy.18
  9.7 1.6 reshape.27
  11.3 1.4 fusion.6
  12.7 81.3 %all-gather.3.cloned.1.call-done = bf16[32,100,2048]{2,1,0:T(8,128)(2,1)} async-done(((bf16[2,100,2048]{2,1,0:T(8,128)(2,1)}), bf16[32,100,2048]{2,1,0:T(8,128)(2,1)}) %all-gather.3.cloned.1.call-update) | async-done | bytes 13107216 | tf_op jit(solution)/shard_map/all_gather | solution.py:56
  93.9 22.6 %fusion.15 = (f32[32]{0:T(128)S(1)}, f32[2,32]{1,0:T(2,128)}) fusion(bf16[32,100,2048]{2,1,0:T(8,128)(2,1)} %all-gather.3.cloned.1.call-done, bf16[2,100,2048]{2,1,0:T(8,128)(2,1)} %fusion.6), kind=kOutput, calls=%fused_computation.22 | convolution fusion | flops 26214432 | bytes 13926784 | tf_op jit(solution)/shard_map/dot_general | solution.py:58
  116.5 3.8 %psum.35 = f32[32]{0:T(128)S(1)} all-reduce(f32[32]{0:T(128)S(1)} %get-tuple-element.5), channel_id=1, replica_groups=mesh['blk_0'=2,'blk_1'=4,'blk_2'=2,'walk_0'=2,'walk_1'=8] {'blk_0'}, use_global_device_ids=true, to_apply=%region_1.0 | all-reduce | flops 32 | bytes 256 | tf_op jit(solution)/shard_map/psum | solution.py:16
  120.3 8.4 %psum.36 = f32[32]{0:T(128)S(1)} all-reduce(f32[32]{0:T(128)S(1)} %psum.35), channel_id=1, replica_groups=mesh['blk_0'=2,'blk_1'=4,'blk_2'=2,'walk_0'=2,'walk_1'=8] {'blk_1'}, use_global_device_ids=true, to_apply=%region_2.0 | all-reduce | flops 32 | bytes 256 | tf_op jit(solution)/shard_map/psum | solution.py:16
  128.7 5.5 %psum.37 = f32[32]{0:T(128)S(1)} all-reduce(f32[32]{0:T(128)S(1)} %psum.36), channel_id=1, replica_groups=mesh['blk_0'=2,'blk_1'=4,'blk_2'=2,'walk_0'=2,'walk_1'=8] {'blk_2'}, use_global_device_ids=true, to_apply=%region_3.0 | all-reduce | flops 32 | bytes 256 | tf_op jit(solution)/shard_map/psum | solution.py:16
  134.2 5.3 %psum.38 = f32[32]{0:T(128)S(1)} all-reduce(f32[32]{0:T(128)S(1)} %psum.37), channel_id=1, replica_groups=mesh['blk_0'=2,'blk_1'=4,'blk_2'=2,'walk_0'=2,'walk_1'=8] {'walk_0'}, use_global_device_ids=true, to_apply=%region_4.0 | all-reduce | flops 32 | bytes 256 | tf_op jit(solution)/shard_map/psum | solution.py:16
  139.5 13.7 %psum.39 = f32[32]{0:T(128)S(1)} all-reduce(f32[32]{0:T(128)S(1)} %psum.38), channel_id=1, replica_groups=mesh['blk_0'=2,'blk_1'=4,'blk_2'=2,'walk_0'=2,'walk_1'=8] {'walk_1'}, use_global_device_ids=true, to_apply=%region_5.0 | all-reduce | flops 32 | bytes 256 | tf_op jit(solution)/shard_map/psum | solution.py:16
  153.2 0.5 fusion.14
  153.7 3.7 %fusion.10 = f32[1,128,2048]{2,0,1:T(1,128)S(1)} fusion(bf16[2,128,2048]{2,1,0:T(8,128)(2,1)S(1)} %copy-done, f32[32]{0:T(128)S(1)} %get-tuple-element.3, s32[]{:T(128)S(6)} %select_n.3), kind=kOutput, calls=%fused_computation.15 | convolution fusion | flops 6291456 | bytes 2097284 | tf_op jit(solution)/shard_map/dot_general | solution.py:66
  157.4 0.7 copy.25
  158.2 0.1 bitcast_multiply_fusion
  158.3 0.3 copy.21
  158.6 27.7 %all_to_all.10 = f32[16,128,128]{2,1,0:T(8,128)S(1)} all-to-all(f32[16,128,128]{2,1,0:T(8,128)S(1)} %copy.21), channel_id=1, replica_groups=mesh['blk_0'=2,'blk_1'=4,'blk_2'=2,'walk_0'=2,'walk_1'=8] {'walk_0','wal..., dimensions={0} | all-to-all | bytes 2097152 | tf_op jit(solution)/shard_map/all_to_all | solution.py:26
  186.4 0.1 copy.22
  186.5 0.1 broadcast_in_dim.2
  186.6 19.3 %all_to_all.11 = bf16[16,128,128]{1,2,0:T(8,128)(2,1)} all-to-all(bf16[16,128,128]{1,2,0:T(8,128)(2,1)S(1)} %broadcast_in_dim.2), channel_id=1, replica_groups=mesh['blk_0'=2,'blk_1'=4,'blk_2'=2,'walk_0'=2,'walk_1'=8] {'walk_0','wal..., dimensions={0} | all-to-all | bytes 1048576 | tf_op jit(solution)/shard_map/all_to_all | solution.py:32
  206.0 63.8 %all-gather.5.cloned.1.call-done = bf16[2048,2048]{0,1:T(8,128)(2,1)} async-done(((bf16[128,2048]{0,1:T(8,128)(2,1)}), bf16[2048,2048]{0,1:T(8,128)(2,1)}) %all-gather.5.cloned.1.call-update) | async-done | bytes 8388624 | tf_op jit(solution)/shard_map/all_gather | solution.py:71
  269.8 7.5 %convolution_convert_fusion = bf16[2048,400]{0,1:T(8,128)(2,1)S(1)} fusion(bf16[2048,2048]{0,1:T(8,128)(2,1)} %all-gather.5.cloned.1.call-done, bf16[400,2048]{1,0:T(8,128)(2,1)} %bitcast.41), kind=kOutput, calls=%fused_computation.10 | convolution fusion | flops 3356262400 | bytes 11665408 | tf_op jit(solution)/shard_map/dot_general | solution.py:75
  277.3 3.6 %multiply_convert_fusion.2 = bf16[400,2048]{1,0:T(8,128)(2,1)S(1)} fusion(bf16[2048,400]{0,1:T(8,128)(2,1)S(1)} %convolution_convert_fusion, bf16[2048,2048]{0,1:T(8,128)(2,1)S(1)} %copy-done.4), kind=kOutput, calls=%fused_computation.9 | convolution fusion | flops 3357081600 | bytes 11665408 | tf_op jit(solution)/shard_map/dot_general | solution.py:75
  281.0 3.6 %multiply_convert_fusion.1 = bf16[400,2048]{1,0:T(8,128)(2,1)S(1)} fusion(bf16[400,2048]{1,0:T(8,128)(2,1)S(1)} %multiply_convert_fusion.2, bf16[2048,2048]{0,1:T(8,128)(2,1)S(1)} %copy-done.4), kind=kOutput, calls=%fused_computation.8 | convolution fusion | flops 3357081600 | bytes 11665408 | tf_op jit(solution)/shard_map/dot_general | solution.py:75
  284.6 5.2 %fusion.5 = bf16[400,2048]{1,0:T(8,128)(2,1)} fusion(bf16[2048,400]{0,1:T(8,128)(2,1)S(1)} %convolution_convert_fusion, bf16[400,2048]{1,0:T(8,128)(2,1)S(1)} %multiply_convert_fusion.1, bf16[400,2048]{1,0:T(8,128)(2,1)S(1)} %multiply_convert_fusion.2, bf16[400,2048]{1,0:T(8,128)(2,1)S(1)} %bitcast.42, bf16[2048,2048]{0,1:T(8,128)(2,1)S(1)} %copy-done.4), kind=kOutput, calls=%fused_computation.6 | convolution fusion | flops 3365273600 | bytes 16580608 | tf_op jit(solution)/shard_map/dot_general | solution.py:75
  (15 shorter events, 0.2 us)
Async XLA Ops:
  7.2 146.5 %copy-start = (bf16[2,128,2048]{2,1,0:T(8,128)(2,1)S(1)}, bf16[2,128,2048]{2,1,0:T(8,128)(2,1)}, u32[]{:S(2)}) copy-start(bf16[2,128,2048]{2,1,0:T(8,128)(2,1)} %param.8) | copy-start | bytes 3145732
  7.2 4.1 %copy-start.2 = (bf16[2,2,100,100]{3,1,2,0:T(2,128)(2,1)S(1)}, bf16[2,2,100,100]{3,1,2,0:T(2,128)(2,1)}, u32[]{:S(2)}) copy-start(bf16[2,2,100,100]{3,1,2,0:T(2,128)(2,1)} %param.6) | copy-start | bytes 240004
  7.2 86.7 %all-gather.3.cloned.1.call-start = ((), (), s32[]{:S(2)}) async-start(), calls=%async_computation.2 | async-start | bytes 14483456 | tf_op jit(solution)/shard_map/all_gather | solution.py:56
  9.7 260.1 %all-gather.5.cloned.1.call-start = ((), (), s32[]{:S(2)}) async-start(), calls=%async_computation.3 | async-start | bytes 8912896 | tf_op jit(solution)/shard_map/all_gather | solution.py:71
  12.7 140.5 %copy-start.3 = (f32[32]{0:T(128)S(1)}, f32[32]{0:T(128)}, u32[]{:S(2)}) copy-start(f32[32]{0:T(128)} %param.9) | copy-start | bytes 388
  269.8 7.6 %copy-start.4 = (bf16[2048,2048]{0,1:T(8,128)(2,1)S(1)}, bf16[2048,2048]{0,1:T(8,128)(2,1)}, u32[]{:S(2)}) copy-start(bf16[2048,2048]{0,1:T(8,128)(2,1)} %all-gather.5.cloned.1.call-done) | copy-start | bytes 25165828
  280.9 3.6 %copy-start.1 = (bf16[2,200,2048]{2,1,0:T(8,128)(2,1)S(1)}, bf16[2,200,2048]{2,1,0:T(8,128)(2,1)}, u32[]{:S(2)}) copy-start(bf16[2,200,2048]{2,1,0:T(8,128)(2,1)} %param.5) | copy-start | bytes 4915204
Sparse Core Ops, SparseCore 0:
  10.4 83.4 all-gather.2
  206.1 63.6 all-gather.4
where the time goes:
time: 297 us
  waiting for transfers between devices  145 us (49%)
  blocking collectives  83.7 us (28%)
  matrix products  47.6 us (16%)
  between operations  14.2 us (5%)
  local copies, waits for them, and re-layouts  5.29 us (2%)
    all_gather x1, waiting for transfers between devices, local(): piece = lax.all_gather(rotated_chol, BLK, axis=0, tiled=True)  81.3 us
    all_gather x1, waiting for transfers between devices, local(): field = lax.all_gather(row_block, BLK, axis=0, tiled=True)  63.8 us
    psum x5, blocking collectives, by_axis(): return functools.reduce(lax.psum, axes, array)  36.6 us
    all_to_all x1, blocking collectives, sent_and_summed(): lax.all_to_all(blocks, axis, split_axis=0, concat_axis=0, tiled=True)  27.7 us
    dot_general x1, matrix products, local(): lax.dot_general(flat_theta, flat_piece, (((1,), (1,)), ((), ())), preferr...  22.6 us
    dot_general x4, matrix products, local(): jnp.dot(current, field, preferred_element_type=jnp.float32) / order  19.9 us
    all_to_all x1, blocking collectives, sent_to_all(): lax.all_to_all(jnp.broadcast_to(array[None], (count, *array.shape)), axis...  19.3 us
  transfers between devices with their start and end apart: 2, of which 2 were waited for; matrix products, arithmetic and copies ran while one was open for 1% of the time, Pallas kernels for 0%

commit v1 on v0

--- a/solution.py
+++ b/solution.py
@@ -10,6 +10,11 @@
 WALK = ("walk_0", "walk_1")
 BLK_WALK = ("blk_0", "blk_1", "blk_2", "walk_0", "walk_1")
 time_root = 0.1
+
+
+def slices_spread(raw):
+    back = lax.all_to_all(jnp.stack(lax.axis_size(BLK) * [raw], 0), BLK, 0, 0)
+    return jnp.concatenate(back, 0)
 
 
 def by_axis(array, axes):
@@ -68,7 +73,7 @@
     )
     narrow = sent_and_summed(partial_value, WALK, 1).astype(jnp.bfloat16)
     row_block = gather_directly(narrow, WALK, 1)
-    field = lax.all_gather(row_block, BLK, axis=0, tiled=True)
+    field = slices_spread(row_block)
     current = walkers.reshape(wdev_count * double_rows, orbitals)
     total = current.astype(jnp.float32)
     for order in range(1, 5):

time: 297 us -> 334 us (1.12)
  blocking collectives: 83.7 us -> 187 us
  waiting for transfers between devices: 145 us -> 81.3 us
  matrix products: 47.6 us -> 43.6 us
    all_to_all x0 -> x1, blocking collectives: none -> 103 us  [slices_spread(): back = lax.all_to_all(jnp.stack(lax.axis_size(BLK) * [raw], 0), BLK, 0, 0)]
    all_gather x1 -> x0, waiting for transfers between devices: 63.8 us -> none  [local(): field = lax.all_gather(row_block, BLK, axis=0, tiled=True)]
    dot_general x4, matrix products: 19.9 us -> 15.9 us  [local(): jnp.dot(current, field, preferred_element_type=jnp.float32) / order]
  transfers between devices with their start and end apart: 2 -> 1, of which waited for: 2 -> 1; matrix products, arithmetic and copies ran while one was open for 1% -> 1% of each run, Pallas kernels for 0% -> 0%
where the time goes in v1:
time: 334 us; the launch traced here: 333 us
  blocking collectives  187 us (56%)
  waiting for transfers between devices  81.3 us (24%)
  matrix products  43.6 us (13%)
  between operations  14.2 us (4%)
  local copies, waits for them, and re-layouts  6.56 us (2%)
    all_to_all x1, blocking collectives, slices_spread(): back = lax.all_to_all(jnp.stack(lax.axis_size(BLK) * [raw], 0), BLK, 0, 0)  103 us
    all_gather x1, waiting for transfers between devices, local(): piece = lax.all_gather(rotated_chol, BLK, axis=0, tiled=True)  81.3 us
    psum x5, blocking collectives, by_axis(): return functools.reduce(lax.psum, axes, array)  36.6 us
    all_to_all x1, blocking collectives, sent_and_summed(): lax.all_to_all(blocks, axis, split_axis=0, concat_axis=0, tiled=True)  27.7 us
    dot_general x1, matrix products, local(): lax.dot_general(flat_theta, flat_piece, (((1,), (1,)), ((), ())), preferr...  22.6 us
    all_to_all x1, blocking collectives, sent_to_all(): lax.all_to_all(jnp.broadcast_to(array[None], (count, *array.shape)), axis...  19.2 us
    dot_general x4, matrix products, local(): jnp.dot(current, field, preferred_element_type=jnp.float32) / order  15.9 us
  transfers between devices with their start and end apart: 1, of which 1 were waited for; matrix products, arithmetic and copies ran while one was open for 1% of the time, Pallas kernels for 0%

profile of v1, /device:TPU:1, one launch (start us, length us, event | category | flops | bytes accessed | tf_op | source)
XLA Modules:
  0.0 333.2 jit_solution(5296502653791872378)
XLA Ops:
  7.2 2.4 copy.21
  9.7 1.6 reshape.29
  11.3 1.4 fusion.6
  12.6 81.3 %all-gather.2.cloned.1.call-done = bf16[32,100,2048]{2,1,0:T(8,128)(2,1)} async-done(((bf16[2,100,2048]{2,1,0:T(8,128)(2,1)}), bf16[32,100,2048]{2,1,0:T(8,128)(2,1)}) %all-gather.2.cloned.1.call-update) | async-done | bytes 13107216 | tf_op jit(solution)/shard_map/all_gather | solution.py:61
  93.9 22.6 %fusion.15 = (f32[32]{0:T(128)S(1)}, f32[2,32]{1,0:T(2,128)}) fusion(bf16[32,100,2048]{2,1,0:T(8,128)(2,1)} %all-gather.2.cloned.1.call-done, bf16[2,100,2048]{2,1,0:T(8,128)(2,1)} %fusion.6), kind=kOutput, calls=%fused_computation.22 | convolution fusion | flops 26214432 | bytes 13926784 | tf_op jit(solution)/shard_map/dot_general | solution.py:63
  116.5 3.8 %psum.35 = f32[32]{0:T(128)S(1)} all-reduce(f32[32]{0:T(128)S(1)} %get-tuple-element.5), channel_id=1, replica_groups=mesh['blk_0'=2,'blk_1'=4,'blk_2'=2,'walk_0'=2,'walk_1'=8] {'blk_0'}, use_global_device_ids=true, to_apply=%region_1.0 | all-reduce | flops 32 | bytes 256 | tf_op jit(solution)/shard_map/psum | solution.py:21
  120.3 8.4 %psum.36 = f32[32]{0:T(128)S(1)} all-reduce(f32[32]{0:T(128)S(1)} %psum.35), channel_id=1, replica_groups=mesh['blk_0'=2,'blk_1'=4,'blk_2'=2,'walk_0'=2,'walk_1'=8] {'blk_1'}, use_global_device_ids=true, to_apply=%region_2.0 | all-reduce | flops 32 | bytes 256 | tf_op jit(solution)/shard_map/psum | solution.py:21
  128.7 5.5 %psum.37 = f32[32]{0:T(128)S(1)} all-reduce(f32[32]{0:T(128)S(1)} %psum.36), channel_id=1, replica_groups=mesh['blk_0'=2,'blk_1'=4,'blk_2'=2,'walk_0'=2,'walk_1'=8] {'blk_2'}, use_global_device_ids=true, to_apply=%region_3.0 | all-reduce | flops 32 | bytes 256 | tf_op jit(solution)/shard_map/psum | solution.py:21
  134.2 5.3 %psum.38 = f32[32]{0:T(128)S(1)} all-reduce(f32[32]{0:T(128)S(1)} %psum.37), channel_id=1, replica_groups=mesh['blk_0'=2,'blk_1'=4,'blk_2'=2,'walk_0'=2,'walk_1'=8] {'walk_0'}, use_global_device_ids=true, to_apply=%region_4.0 | all-reduce | flops 32 | bytes 256 | tf_op jit(solution)/shard_map/psum | solution.py:21
  139.5 13.7 %psum.39 = f32[32]{0:T(128)S(1)} all-reduce(f32[32]{0:T(128)S(1)} %psum.38), channel_id=1, replica_groups=mesh['blk_0'=2,'blk_1'=4,'blk_2'=2,'walk_0'=2,'walk_1'=8] {'walk_1'}, use_global_device_ids=true, to_apply=%region_5.0 | all-reduce | flops 32 | bytes 256 | tf_op jit(solution)/shard_map/psum | solution.py:21
  153.2 0.5 fusion.14
  153.7 3.7 %fusion.10 = f32[1,128,2048]{2,0,1:T(1,128)S(1)} fusion(bf16[2,128,2048]{2,1,0:T(8,128)(2,1)S(1)} %copy-done, f32[32]{0:T(128)S(1)} %get-tuple-element.3, s32[]{:T(128)S(6)} %select_n.3), kind=kOutput, calls=%fused_computation.15 | convolution fusion | flops 6291456 | bytes 2097284 | tf_op jit(solution)/shard_map/dot_general | solution.py:71
  157.4 0.7 copy.29
  158.3 0.3 copy.24
  158.6 27.7 %all_to_all.15 = f32[16,128,128]{2,1,0:T(8,128)S(1)} all-to-all(f32[16,128,128]{2,1,0:T(8,128)S(1)} %copy.24), channel_id=1, replica_groups=mesh['blk_0'=2,'blk_1'=4,'blk_2'=2,'walk_0'=2,'walk_1'=8] {'walk_0','wal..., dimensions={0} | all-to-all | bytes 2097152 | tf_op jit(solution)/shard_map/all_to_all | solution.py:31
  186.4 0.1 copy.25
  186.6 19.2 %all_to_all.16 = bf16[16,128,128]{1,2,0:T(8,128)(2,1)S(1)} all-to-all(bf16[16,128,128]{1,2,0:T(8,128)(2,1)S(1)} %broadcast_in_dim.2), channel_id=1, replica_groups=mesh['blk_0'=2,'blk_1'=4,'blk_2'=2,'walk_0'=2,'walk_1'=8] {'walk_0','wal..., dimensions={0} | all-to-all | bytes 1048576 | tf_op jit(solution)/shard_map/all_to_all | solution.py:37
  205.8 0.2 copy.26
  206.1 1.1 stack.3
  207.1 103.2 %all_to_all.17 = bf16[16,128,2048]{2,1,0:T(8,128)(2,1)S(1)} all-to-all(bf16[16,128,2048]{2,1,0:T(8,128)(2,1)S(1)} %stack.3), channel_id=1, replica_groups=mesh['blk_0'=2,'blk_1'=4,'blk_2'=2,'walk_0'=2,'walk_1'=8] {'blk_0','blk_..., dimensions={0} | all-to-all | bytes 16777216 | tf_op jit(solution)/shard_map/all_to_all | solution.py:16
  310.4 3.6 %convolution_convert_fusion = bf16[2048,400]{0,1:T(8,128)(2,1)S(1)} fusion(bf16[400,2048]{1,0:T(8,128)(2,1)S(1)} %bitcast.46, bf16[2048,2048]{1,0:T(8,128)(2,1)S(1)} %bitcast.40), kind=kOutput, calls=%fused_computation.10 | convolution fusion | flops 3356262400 | bytes 11665408 | tf_op jit(solution)/shard_map/dot_general | solution.py:80
  314.0 3.6 %multiply_convert_fusion.2 = bf16[400,2048]{1,0:T(8,128)(2,1)S(1)} fusion(bf16[2048,400]{0,1:T(8,128)(2,1)S(1)} %convolution_convert_fusion, bf16[2048,2048]{1,0:T(8,128)(2,1)S(1)} %bitcast.41), kind=kOutput, calls=%fused_computation.9 | convolution fusion | flops 3357081600 | bytes 11665408 | tf_op jit(solution)/shard_map/dot_general | solution.py:80
  317.6 3.6 %multiply_convert_fusion.1 = bf16[400,2048]{1,0:T(8,128)(2,1)S(1)} fusion(bf16[400,2048]{1,0:T(8,128)(2,1)S(1)} %multiply_convert_fusion.2, bf16[2048,2048]{1,0:T(8,128)(2,1)S(1)} %bitcast.42), kind=kOutput, calls=%fused_computation.8 | convolution fusion | flops 3357081600 | bytes 11665408 | tf_op jit(solution)/shard_map/dot_general | solution.py:80
  321.2 5.1 %fusion.5 = bf16[400,2048]{1,0:T(8,128)(2,1)} fusion(bf16[2048,400]{0,1:T(8,128)(2,1)S(1)} %convolution_convert_fusion, bf16[400,2048]{1,0:T(8,128)(2,1)S(1)} %multiply_convert_fusion.1, bf16[400,2048]{1,0:T(8,128)(2,1)S(1)} %multiply_convert_fusion.2, bf16[400,2048]{1,0:T(8,128)(2,1)S(1)} %bitcast.47, bf16[2048,2048]{1,0:T(8,128)(2,1)S(1)} %bitcast.43), kind=kOutput, calls=%fused_computation.6 | convolution fusion | flops 3365273600 | bytes 16580608 | tf_op jit(solution)/shard_map/dot_general | solution.py:80
  (13 shorter events, 0.3 us)
Async XLA Ops:
  7.2 146.5 %copy-start = (bf16[2,128,2048]{2,1,0:T(8,128)(2,1)S(1)}, bf16[2,128,2048]{2,1,0:T(8,128)(2,1)}, u32[]{:S(2)}) copy-start(bf16[2,128,2048]{2,1,0:T(8,128)(2,1)} %param.8) | copy-start | bytes 3145732
  7.2 4.1 %copy-start.2 = (bf16[2,2,100,100]{3,1,2,0:T(2,128)(2,1)S(1)}, bf16[2,2,100,100]{3,1,2,0:T(2,128)(2,1)}, u32[]{:S(2)}) copy-start(bf16[2,2,100,100]{3,1,2,0:T(2,128)(2,1)} %param.6) | copy-start | bytes 240004
  7.2 86.7 %all-gather.2.cloned.1.call-start = ((), (), s32[]{:S(2)}) async-start(), calls=%async_computation.3 | async-start | bytes 14483456 | tf_op jit(solution)/shard_map/all_gather | solution.py:61
  12.6 140.6 %copy-start.3 = (f32[32]{0:T(128)S(1)}, f32[32]{0:T(128)}, u32[]{:S(2)}) copy-start(f32[32]{0:T(128)} %param.9) | copy-start | bytes 388
  207.1 103.2 %copy-start.1 = (bf16[2,200,2048]{2,1,0:T(8,128)(2,1)S(1)}, bf16[2,200,2048]{2,1,0:T(8,128)(2,1)}, u32[]{:S(2)}) copy-start(bf16[2,200,2048]{2,1,0:T(8,128)(2,1)} %param.5) | copy-start | bytes 4915204
Sparse Core Ops, SparseCore 0:
  10.4 83.4 all-gather.1
